TPU v7x, 32 devices: a whole 2x2x4 slice. The times are simulated.
32 devices in a mesh: seq: 16 (over z, y, x), tp: 2 (over core).
Axes of the slice: x: 2, y: 2, z: 4, core: 2. Of those that a mesh axis runs over, the one named last changes fastest.
Arguments:
- img: bfloat16 [4, 512, 3072], P(None, 'seq', 'tp'), may hold values from -6 to 6
- txt: bfloat16 [4, 64, 3072], P(None, 'seq', 'tp'), may hold values from -6 to 6
- prev_mod: bfloat16 [4, 512, 3072], P(None, 'seq', 'tp'), may hold values from -47 to 47
- cache: float32 [4, 512, 3072], P(None, 'seq', 'tp'), may hold values from -6 to 6
- modulation: bfloat16 [3, 4, 3072], P(None, None, 'tp'), may hold values from -4 to 4
- w_qkv: bfloat16 [3072, 3, 2048], P('seq', None, 'tp'), may hold values from -1 to 1, as said below
- qk_gain: float32 [2, 2048], P(None, 'tp'), may hold values from 0.5 to 6, as said below
- output_weight: bfloat16 [2048, 3072], P('tp'), may hold values from -0.1875 to 0.1875
- text_len: int32 [4], replicated, may hold values from 1 to 64
- refresh: int32 [4], replicated, may hold values from 0 to 1, as said below
Outputs:
- out_img: float32 [4, 512, 3072], P(None, 'seq', 'tp')
- new_cache: float32 [4, 512, 3072], P(None, 'seq', 'tp')
- rel_l1: float32 [4], replicated
Inputs may be any that keep to these rules, and one draw needn't show every extreme that they name: `refresh`: at least one sequence has flag 1 and at least one has flag 0. `w_qkv`: entries of spread about one over the square root of 3072. `qk_gain`: positive.
All inputs are finite; a program needn't handle non-finite values.
Results may differ from a plain program's by a relative error of at most 0.013.
The roundings to bfloat16 on the way count: a program that leaves them out, or rounds other values in their place, can miss the bound.
Values may be sent and summed in bfloat16 or wider, within the bound.
A program may use at most 128 MiB of HBM per device.

v0:
```python
import jax
import jax.numpy as jnp
from jax import lax
from jax.sharding import PartitionSpec as P

HD = 128


EPS = 0.1
NEG = -1e30


def unit_heads(block, gain):
    shaped = block.reshape(block.shape[:-1] + (block.shape[-1] // HD, HD))
    scaled = shaped * lax.rsqrt(jnp.mean(jnp.square(shaped), axis=-1, keepdims=True) + EPS)
    return scaled.reshape(block.shape) * gain


def local(img, txt, prev_mod, cache, modulation, w_qkv, qk_gain, output_weight, text_len, refresh):
    batch, img_rows, width_loc = img.shape
    txt_rows = txt.shape[1]
    rows = txt_rows + img_rows
    joined = jnp.concatenate([txt, img], axis=1)
    local_mods = modulation.astype(jnp.float32)
    wide, wide_mod = (
        lax.all_gather(joined, "tp", axis=2, tiled=True),
        lax.all_gather(modulation, "tp", axis=2, tiled=True),
    )
    wide_mods = wide_mod.astype(jnp.float32)
    values = wide.astype(jnp.float32)
    center = jnp.mean(values, axis=2, keepdims=True)
    spread = jnp.mean(jnp.square(values - center), axis=2, keepdims=True)
    normed = (values - center) * lax.rsqrt(spread + EPS)
    modded = (normed * (1.0 + wide_mods[1][:, None, :]) + wide_mods[0][:, None, :]).astype(
        jnp.bfloat16
    )
    offset = lax.axis_index("tp") * width_loc
    own_image = lax.dynamic_slice_in_dim(modded[:, txt_rows:, :], offset, width_loc, 2)
    previous = prev_mod.astype(jnp.float32)
    gap = jnp.sum(jnp.abs(own_image.astype(jnp.float32) - previous), axis=(1, 2))
    base_sum = jnp.sum(jnp.abs(previous), axis=(1, 2))
    numer, denom = lax.psum((gap, base_sum), ("seq", "tp"))
    rel_l1 = numer / jnp.maximum(denom, 1.0)
    columns = w_qkv.shape[2]
    projected = jnp.einsum(
        "btd,dkc->btkc",
        modded,
        lax.all_gather(w_qkv, "seq", axis=0, tiled=True),
        preferred_element_type=jnp.float32,
    )
    heads = columns // HD
    query = unit_heads(projected[:, txt_rows:, 0, :], qk_gain[0]).astype(jnp.bfloat16)
    query_heads = query.reshape(batch, img_rows, heads, HD)
    keyed = unit_heads(projected[:, :, 1, :], qk_gain[1]).astype(jnp.bfloat16)
    valued = projected[:, :, 2, :].astype(jnp.bfloat16)
    paired = jnp.stack([keyed, valued], axis=2)
    score_scale = 1.0 / HD**0.5
    start_top = jnp.full((batch, heads, img_rows), NEG, jnp.float32)
    piece = lax.all_gather(paired, "seq", axis=1, tiled=True)
    top = start_top
    count = piece.shape[1]
    index = jnp.arange(count, dtype=jnp.int32)
    slot = index % rows
    text_pos = index // rows * txt_rows + slot
    valid = (slot >= txt_rows)[None, :] | (text_pos[None, :] < text_len[:, None])
    keys = piece[:, :, 0, :].reshape(batch, count, heads, HD)
    vals = piece[:, :, 1, :].reshape(batch, count, heads, HD)
    logit_scores = (
        jnp.einsum("bqhc,bkhc->bhqk", query_heads, keys, preferred_element_type=jnp.float32)
        * score_scale
    )
    logit_scores = jnp.where(valid[:, None, None, :], logit_scores, NEG)
    new_top = jnp.maximum(top, jnp.max(logit_scores, axis=3))
    attention_weights = jnp.where(
        valid[:, None, None, :], jnp.exp(logit_scores - new_top[..., None]), 0.0
    )
    total = jnp.sum(attention_weights, axis=3)
    summed_output = jnp.einsum(
        "bhqk,bkhc->bhqc",
        attention_weights.astype(jnp.bfloat16),
        vals,
        preferred_element_type=jnp.float32,
    )
    top, total, summed_output = (new_top, total, summed_output)
    attended_values = (summed_output / total[..., None]).astype(jnp.bfloat16)
    attended_values = attended_values.transpose(0, 2, 1, 3).reshape(batch, img_rows, columns)
    partial_output = jnp.einsum(
        "pxr,ro->pxo", attended_values, output_weight, preferred_element_type=jnp.float32
    )
    whole = lax.psum(partial_output.astype(jnp.bfloat16), "tp").astype(jnp.float32)
    mixed_heads = lax.dynamic_slice_in_dim(whole, lax.axis_index("tp") * width_loc, width_loc, 2)
    resid = local_mods[2][:, None, :] * mixed_heads
    flag = (refresh == 1)[:, None, None]
    new_cache = jnp.where(flag, resid, cache)
    out_img = img.astype(jnp.float32) + new_cache
    return (out_img, new_cache, rel_l1)


def solution(mesh):
    return jax.shard_map(
        local,
        mesh=mesh,
        in_specs=(
            P(None, "seq", "tp"),
            P(None, "seq", "tp"),
            P(None, "seq", "tp"),
            P(None, "seq", "tp"),
            P(None, None, "tp"),
            P("seq", None, "tp"),
            P(None, "tp"),
            P("tp", None),
            P(),
            P(),
        ),
        out_specs=(P(None, "seq", "tp"), P(None, "seq", "tp"), P()),
        check_vma=False,
    )
```

profile of v0, /device:TPU:1, one launch (start us, length us, event | category | flops | bytes accessed | tf_op | source)
XLA Modules:
  0.0 434.5 jit_solution(10169232465015273428)
XLA Ops:
  7.2 0.0 all-gather.3.cloned.1.call-start
  7.2 0.7 all-gather.3.cloned.1.call-update
  7.9 0.0 copy-start.3
  7.9 0.0 all-gather.5.cloned.1.call-start
  8.0 2.1 all_gather.13
  10.0 1.1 pad_maximum_fusion.1
  11.2 2.5 all_gather.12
  13.7 0.2 convert_reduce_fusion
  13.9 0.4 fusion.14
  14.4 0.0 copy-done.3
  14.4 0.5 fusion.17
  14.9 208.0 %all-gather.3.cloned.1.call-done = bf16[3072,3,1024]{2,0,1:T(8,128)(2,1)} async-done(((bf16[192,3,1024]{2,0,1:T(8,128)(2,1)}), bf16[3072,3,1024]{2,0,1:T(8,128)(2,1)}) %all-gather.3.cloned.1.call-update) | async-done | bytes 18874384 | tf_op jit(solution)/shard_map/all_gather | solution.py:48
  222.9 8.1 %fusion = f32[4,36,3,1024]{3,1,2,0:T(8,128)S(1)} fusion(bf16[3072,3,1024]{2,0,1:T(8,128)(2,1)} %all-gather.3.cloned.1.call-done, bf16[4,36,3072]{2,1,0:T(8,128)(2,1)S(1)} %fusion.17), kind=kOutput, calls=%fused_computation | convolution fusion | flops 2717908992 | bytes 21528576 | tf_op jit(solution)/shard_map/btd,dkc->btkc/dot_general | solution.py:45
  231.1 0.9 slice_multiply_fusion
  232.0 0.8 slice.62
  232.7 1.2 reshape.130
  233.9 0.9 reduce_sum.66
  234.8 1.0 copy.47
  235.7 0.1 copy.48
  235.9 1.0 mul.103
  236.9 1.3 mul.104
  238.2 0.4 fusion.51
  238.5 0.0 copy-start.2
  238.5 0.0 copy-start.4
  238.6 1.1 pad_maximum_fusion
  239.7 1.3 copy.50
  240.9 0.0 all-gather.5.cloned.1.call-update
  240.9 0.0 all-reduce.3.cloned.1.call-start
  241.0 1.1 slice.53
  242.1 0.0 copy-done.2
  242.1 1.3 fusion.49
  243.4 41.4 %all-reduce = (f32[4]{0:T(128)S(1)}, f32[4]{0:T(128)S(1)}) all-reduce(f32[4]{0:T(128)S(1)} %get-tuple-element.4, f32[4]{0:T(128)S(1)} %get-tuple-element.3), channel_id=1, replica_groups=mesh['seq'=16,'tp'=2] {'seq','tp'}, use_global_device_ids=true, to_apply=%region_8.9 | all-reduce | flops 8 | bytes 64 | tf_op jit(solution)/shard_map/psum | solution.py:42
  284.8 0.0 copy-done.4
  284.8 0.1 compare_or_fusion
  284.9 0.1 slice.48
  285.0 0.1 copy.66
  285.1 0.2 fusion.52
  285.3 0.2 fusion.54
  285.5 75.8 %all-gather.5.cloned.1.call-done = bf16[4,576,2,1024]{3,0,2,1:T(4,128)(2,1)} async-done(((bf16[4,36,2,1024]{3,0,2,1:T(4,128)(2,1)}), bf16[4,576,2,1024]{3,0,2,1:T(4,128)(2,1)}) %all-gather.5.cloned.1.call-update) | async-done | bytes 9437200 | tf_op jit(solution)/shard_map/all_gather | solution.py:59
  361.3 10.7 %fusion.70 = (bf16[4,576,1,1024]{3,0,2,1:T(4,128)(2,1)}, bf16[4,576,1,1024]{3,0,2,1:T(4,128)(2,1)}) fusion(bf16[4,576,2,1024]{3,0,2,1:T(4,128)(2,1)} %all-gather.5.cloned.1.call-done), kind=kLoop, calls=%fused_computation.82 | loop fusion | bytes 18874368 | tf_op jit(solution)/shard_map/slice | solution.py:66
  372.0 8.0 %reshape.131 = bf16[4,576,8,128]{3,2,0,1:T(8,128)(2,1)} reshape(bf16[4,576,1,1024]{3,0,2,1:T(4,128)(2,1)} %get-tuple-element.9) | data formatting | bytes 9437184 | tf_op jit(solution)/shard_map/reshape;squeeze | solution.py:66
  380.0 7.5 %fusion.13 = (f32[4,8,32]{2,1,0:T(8,128)S(1)}, f32[4,8,32,576]{3,2,1,0:T(8,128)S(1)}) fusion(pred[4,576]{1,0:T(4,128)(4,1)S(1)} %compare_or_fusion, bf16[4,576,8,128]{3,2,0,1:T(8,128)(2,1)} %reshape.131, bf16[4,32,8,128]{3,2,1,0:T(8,128)(2,1)S(1)} %fusion.54), kind=kOutput, calls=%fused_computation.15 | convolution fusion | flops 152763392 | bytes 7346432 | tf_op jit(solution)/shard_map/bqhc,bkhc->bhqk/dot_general | solution.py:69
  387.5 8.0 %reshape.132 = bf16[4,576,8,128]{3,2,0,1:T(8,128)(2,1)} reshape(bf16[4,576,1,1024]{3,0,2,1:T(4,128)(2,1)} %get-tuple-element.10) | data formatting | bytes 9437184 | tf_op jit(solution)/shard_map/reshape;squeeze | solution.py:67
  395.6 0.0 slice-start
  395.6 0.8 fusion.18
  396.4 0.0 slice-start.1
  396.4 8.1 %fusion.41 = bf16[4,8,4,8,128]{4,3,2,1,0:T(8,128)(2,1)S(1)} fusion(bf16[4,576,8,128]{3,2,0,1:T(8,128)(2,1)} %reshape.132, f32[4,8,32,576]{3,2,1,0:T(8,128)S(1)} %get-tuple-element.16, f32[4,8,32]{2,1,0:T(8,128)S(1)} %broadcast_maximum_fusion, pred[4,576]{1,0:T(4,128)(4,1)S(1)} %compare_or_fusion, f32[4,32,8]{1,2,0:T(8,128)S(1)} %bitcast.67), kind=kOutput, calls=%fused_computation.30 | convolution fusion | flops 154206208 | bytes 7350528 | tf_op jit(solution)/shard_map/bhqk,bkhc->bhqc/dot_general | solution.py:78
  404.5 0.0 slice-done
  404.5 0.0 slice-done.1
  404.5 0.0 copy-start.5
  404.5 0.0 copy-start
  404.6 0.0 copy-start.1
  404.6 1.9 fusion.8
  406.4 0.0 all-reduce.3.cloned.1.call-update
  406.5 0.0 copy-done.5
  406.5 0.5 maximum_divide_fusion
  407.0 0.7 bitcast_convert_fusion
  407.7 17.8 %all-reduce.3.cloned.1.call-done = bf16[4,32,3072]{2,1,0:T(8,128)(2,1)} async-done(((bf16[4,32,3072]{2,1,0:T(8,128)(2,1)}), bf16[4,32,3072]{2,1,0:T(8,128)(2,1)}) %all-reduce.3.cloned.1.call-update) | async-done | bytes 786448 | tf_op jit(solution)/shard_map/psum | solution.py:90
  425.5 0.0 copy-done
  425.5 0.0 copy-done.1
  425.5 2.4 convert_add_fusion
  (12 shorter events, 0.1 us)
Async XLA Ops:
  7.2 215.8 %all-gather.3.cloned.1.call-start = ((), (), s32[]{:S(2)}) async-start(), calls=%async_computation | async-start | bytes 20054016 | tf_op jit(solution)/shard_map/all_gather | solution.py:48
  7.9 6.5 %copy-start.3 = (f32[2,1024]{1,0:T(2,128)S(1)}, f32[2,1024]{1,0:T(2,128)}, u32[]{:S(2)}) copy-start(f32[2,1024]{1,0:T(2,128)} %param.16) | copy-start | bytes 24580
  7.9 353.4 %all-gather.5.cloned.1.call-start = ((), (), s32[]{:S(2)}) async-start(), calls=%async_computation.1 | async-start | bytes 10027008 | tf_op jit(solution)/shard_map/all_gather | solution.py:59
  238.5 3.6 copy-start.2
  238.5 46.3 %copy-start.4 = (s32[4]{0:T(128)S(1)}, s32[4]{0:T(128)}, u32[]{:S(2)}) copy-start(s32[4]{0:T(128)} %param.18) | copy-start | bytes 52
  240.9 184.6 %all-reduce.3.cloned.1.call-start = ((), (), s32[]{:S(2)}) async-start(), calls=%async_computation.2 | async-start | bytes 1572864 | tf_op jit(solution)/shard_map/psum | solution.py:90
  395.6 8.9 %slice-start = ((s8[6291456]{0:T(1024)(128)(4,1)}), s8[4194304]{0:T(1024)(128)(4,1)S(1)}, s32[]{:S(2)}) async-start(s8[6291456]{0:T(1024)(128)(4,1)} %bitcast.62), calls=%async_computation.3 | async-start | bytes 8388608
  396.4 8.1 %slice-start.1 = ((s8[6291456]{0:T(1024)(128)(4,1)}), s8[2097152]{0:T(1024)(128)(4,1)S(1)}, s32[]{:S(2)}) async-start(s8[6291456]{0:T(1024)(128)(4,1)} %bitcast.62), calls=%async_computation.4 | async-start | bytes 4194304
  404.5 1.9 copy-start.5
  404.5 21.0 %copy-start = (bf16[4,32,1536]{2,1,0:T(8,128)(2,1)S(1)}, bf16[4,32,1536]{2,1,0:T(8,128)(2,1)}, u32[]{:S(2)}) copy-start(bf16[4,32,1536]{2,1,0:T(8,128)(2,1)} %param.10) | copy-start | bytes 1179652
  404.6 21.0 %copy-start.1 = (f32[4,32,1536]{2,1,0:T(8,128)S(1)}, f32[4,32,1536]{2,1,0:T(8,128)}, u32[]{:S(2)}) copy-start(f32[4,32,1536]{2,1,0:T(8,128)} %param.13) | copy-start | bytes 2359300
Sparse Core Ops, SparseCore 0:
  10.6 212.2 all-gather.2
  241.1 120.1 all-gather.4
  406.6 18.9 all-reduce.2
where the time goes:
time: 436 us; the launch traced here: 434 us
  waiting for transfers between devices  302 us (69%)
  blocking collectives  46 us (11%)
  local copies, waits for them, and re-layouts  34.7 us (8%)
  matrix products  25.6 us (6%)
  between operations  14 us (3%)
  other arithmetic  11.8 us (3%)
    all_gather x1, waiting for transfers between devices, local(): lax.all_gather(w_qkv, 'seq', axis=0, tiled=True)  208 us
    all_gather x1, waiting for transfers between devices, local(): piece = lax.all_gather(paired, 'seq', axis=1, tiled=True)  75.8 us
    psum x1, blocking collectives, local(): numer, denom = lax.psum((gap, base_sum), ('seq', 'tp'))  41.4 us
    psum x1, waiting for transfers between devices, local(): lax.psum(partial_output.astype(jnp.bfloat16), 'tp').astype(jnp.float32)  17.8 us
    slice x1, local copies, waits for them, and re-layouts, local(): keys = piece[:, :, 0, :].reshape(batch, count, heads, HD)  10.7 us
  transfers between devices with their start and end apart: 3, of which 3 were waited for; matrix products, arithmetic and copies ran while one was open for 2% of the time, Pallas kernels for 0%

commit v1 on v0

--- a/solution.py
+++ b/solution.py
@@ -1,9 +1,14 @@
+import functools
+
 import jax
 import jax.numpy as jnp
 from jax import lax
+from jax.experimental import pallas as pl
+from jax.experimental.pallas import tpu as pltpu
 from jax.sharding import PartitionSpec as P
 
 HD = 128
+MESH = pl.DeviceIdType.MESH
 
 
 EPS = 0.1
@@ -96,9 +101,368 @@
     return (out_img, new_cache, rel_l1)
 
 
+def head_kernel(n, dims, chunk_ref, w_ref, wout_ref, gain_ref, mask_ref, rel_ref, mixed_ref, relsum_ref,
+                xbuf, wbuf, woutbuf, qbuf, kvbuf, attsrc, attcat, pbuf, rbuf, relbuf,
+                local_sem, zsend, ssend, fsend, xrecv, diag_recv, wsend, wrecv, wfsend,
+                kvsend, kvrecv, asend, arecv, psend, precv, rsend, rrecv):
+    seq, tp, hloc, cols, half_img, groups = dims
+    planes = seq // cols
+    me = lax.axis_index("seq")
+    t = lax.axis_index("tp")
+    other = 1 - t
+    z = me // cols
+    col = me % cols
+    xp = me + 1 - 2 * (me % 2)
+    yp = me + 2 - 4 * ((me // 2) % 2)
+    rows = chunk_ref.shape[1]
+    width = chunk_ref.shape[2]
+
+    barrier = pltpu.get_barrier_semaphore()
+
+    def greet(k, carry):
+        peer = lax.rem(me * tp + t + k, seq * tp)
+        pl.semaphore_signal(barrier, inc=1, device_id=(peer // tp, peer % tp), device_id_type=MESH)
+        return carry
+
+    lax.fori_loop(1, seq * tp, greet, 0)
+
+    own = pltpu.make_async_copy(chunk_ref, xbuf.at[me], local_sem.at[0])
+    own.start()
+    wout_copy = pltpu.make_async_copy(wout_ref, woutbuf, local_sem.at[1])
+    wout_copy.start()
+    pl.semaphore_wait(barrier, seq * tp - 1)
+
+    def remote(src, dst, send, recv, device):
+        return pltpu.make_async_remote_copy(
+            src_ref=src, dst_ref=dst, send_sem=send, recv_sem=recv,
+            device_id=device, device_id_type=MESH,
+        )
+
+    def arrived(dst, recv):
+        remote(dst, dst, zsend.at[0], recv, (me, other)).wait_recv()
+
+    pending = []
+
+    def launch(copy):
+        copy.start()
+        pending.append(copy)
+
+    for dz in range(1, planes):
+        there = lax.rem(z + dz, planes) * cols + col
+        launch(remote(chunk_ref, xbuf.at[me], zsend.at[dz - 1], xrecv.at[me], (there, t)))
+    launch(remote(chunk_ref, xbuf.at[me], ssend.at[0, 0], xrecv.at[me], (xp, t)))
+    launch(remote(chunk_ref, xbuf.at[me], ssend.at[0, 1], xrecv.at[me], (yp, t)))
+
+    wcore = me % 2
+    for k in range(hloc):
+        hl = lax.rem(me + k, hloc)
+        head = t * hloc + hl
+        same = jnp.logical_and(head == me, wcore == t)
+
+        @pl.when(same)
+        def _():
+            pltpu.make_async_copy(w_ref.at[hl], wbuf.at[me], wrecv.at[me]).start()
+
+        @pl.when(jnp.logical_not(same))
+        def _():
+            remote(w_ref.at[hl], wbuf.at[me], wsend.at[k], wrecv.at[me], (head, wcore)).start()
+
+    for dz in range(1, planes):
+        src = lax.rem(z + dz, planes) * cols + col
+        arrived(xbuf.at[src], xrecv.at[src])
+        launch(remote(xbuf.at[src], xbuf.at[src], ssend.at[dz, 0], xrecv.at[src], (xp, t)))
+        launch(remote(xbuf.at[src], xbuf.at[src], ssend.at[dz, 1], xrecv.at[src], (yp, t)))
+
+    for dz in range(planes):
+        plane = lax.rem(z + dz, planes)
+        sx = plane * cols + xp % cols
+        sy = plane * cols + yp % cols
+        arrived(xbuf.at[sx], xrecv.at[sx])
+        launch(remote(xbuf.at[sx, 0], xbuf.at[sx, 0], fsend.at[dz, 0], diag_recv.at[plane, 0], (yp, t)))
+        arrived(xbuf.at[sy], xrecv.at[sy])
+        launch(remote(xbuf.at[sy, 1], xbuf.at[sy, 1], fsend.at[dz, 1], diag_recv.at[plane, 1], (xp, t)))
+
+    for k in range(seq // 2):
+        slot = 2 * k + t
+        arrived(wbuf.at[slot], wrecv.at[slot])
+        launch(remote(wbuf.at[slot], wbuf.at[slot], wfsend.at[k], wrecv.at[slot], (me, other)))
+
+    def send_rel(k, carry):
+        peer = lax.rem(me * tp + t + k, seq * tp)
+        remote(rel_ref, relbuf.at[me * tp + t], rsend.at[k], rrecv.at[me * tp + t],
+               (peer // tp, peer % tp)).start()
+        return carry
+
+    lax.fori_loop(1, seq * tp, send_rel, 0)
+
+    for k in range(seq // 2):
+        slot = 2 * k + other
+        arrived(wbuf.at[slot], wrecv.at[slot])
+    own.wait()
+    for plane in range(planes):
+        sd = plane * cols + cols - 1 - col
+        for half in range(2):
+            arrived(xbuf.at[sd, half], diag_recv.at[plane, half])
+
+    per = seq // groups
+    gq = gain_ref[0:1, :]
+    gk = gain_ref[1:2, :]
+
+    def unit(block, gain):
+        return (block * lax.rsqrt(jnp.mean(jnp.square(block), axis=1, keepdims=True) + EPS) * gain).astype(jnp.bfloat16)
+
+    def kv_copy(g):
+        part = kvbuf.at[t, pl.ds(g * per, per)]
+        return remote(part, part, kvsend.at[g], kvrecv.at[g], (me, other))
+
+    hs = seq // 2
+    for g in range(groups):
+        s0 = g * per
+        total = jnp.dot(
+            xbuf[s0:s0 + per, 0].reshape(per * rows, width),
+            wbuf[:hs].reshape(width, 3 * HD), preferred_element_type=jnp.float32)
+        total = total + jnp.dot(
+            xbuf[s0:s0 + per, 1].reshape(per * rows, width),
+            wbuf[hs:].reshape(width, 3 * HD), preferred_element_type=jnp.float32)
+        q = unit(total[:, :HD], gq)
+        qbuf[s0:s0 + per] = q.reshape(per, rows, HD)
+        k = unit(total[:, HD:2 * HD], gk)
+        v = total[:, 2 * HD:].astype(jnp.bfloat16)
+        kvbuf[t, s0:s0 + per, 0] = k.reshape(per, rows, HD)
+        kvbuf[t, s0:s0 + per, 1] = v.reshape(per, rows, HD)
+        launch(kv_copy(g))
+    for g in range(groups):
+        part = kvbuf.at[other, pl.ds(g * per, per)]
+        arrived(part, kvrecv.at[g])
+
+    text = n * half_img
+    for i in range(n):
+        lo, hi = i * half_img, (i + 1) * half_img
+
+        def keys(kind):
+            parts = []
+            for c in range(2):
+                parts.append(kvbuf[c, :, kind, lo:hi, :].reshape(seq * half_img, HD))
+                parts.append(kvbuf[c, :, kind, text:, :].reshape(seq * (rows - text), HD))
+            return jnp.concatenate(parts, axis=0)
+
+        q = qbuf[:, lo:hi, :].reshape(seq * half_img, HD)
+        scores = lax.dot_general(q, keys(0), (((1,), (1,)), ((), ())),
+                                 preferred_element_type=jnp.float32) * (1.0 / HD**0.5)
+        valid = mask_ref[i:i + 1, :] > 0.0
+        scores = jnp.where(valid, scores, NEG)
+        top = jnp.max(scores, axis=1, keepdims=True)
+        weights = jnp.where(valid, jnp.exp(scores - top), 0.0)
+        total = jnp.sum(weights, axis=1, keepdims=True)
+        summed = jnp.dot(weights.astype(jnp.bfloat16), keys(1), preferred_element_type=jnp.float32)
+        attsrc[:, lo:hi, :] = (summed / total).astype(jnp.bfloat16).reshape(seq, half_img, HD)
+
+    home = me // hloc
+    hl = me % hloc
+    mine = attcat.at[pl.ds(pl.multiple_of(t * text, half_img), text), pl.ds(pl.multiple_of(hl * HD, HD), HD)]
+    for k in range(seq):
+        s = lax.rem(me + k, seq)
+        if k == 0:
+            same = home == t
+
+            @pl.when(same)
+            def _():
+                pltpu.make_async_copy(attsrc.at[s], mine, arecv.at[hl * 2 + t]).start()
+
+            @pl.when(jnp.logical_not(same))
+            def _():
+                remote(attsrc.at[s], mine, asend.at[k], arecv.at[hl * 2 + t], (s, home)).start()
+        else:
+            launch(remote(attsrc.at[s], mine, asend.at[k], arecv.at[hl * 2 + t], (s, home)))
+    wout_copy.wait()
+    for h in range(hloc):
+        for c in range(2):
+            arrived(attcat.at[pl.ds(c * text, text), pl.ds(h * HD, HD)], arecv.at[h * 2 + c])
+
+    out_width = mixed_ref.shape[1]
+    acts = attcat[...]
+    theirs = jnp.dot(acts, woutbuf[:, pl.ds(pl.multiple_of(other * out_width, 128), out_width)],
+                     preferred_element_type=jnp.float32)
+    pbuf[...] = theirs.astype(jnp.bfloat16)
+    give = remote(pbuf, rbuf, psend.at[0], precv.at[0], (me, other))
+    launch(give)
+    ours = jnp.dot(acts, woutbuf[:, pl.ds(pl.multiple_of(t * out_width, 128), out_width)],
+                   preferred_element_type=jnp.float32)
+
+    relbuf[me * tp + t] = rel_ref[...]
+
+    def wait_rel(k, carry):
+        peer = lax.rem(me * tp + t + k, seq * tp)
+        arrived(relbuf.at[peer], rrecv.at[peer])
+        remote(rel_ref, relbuf.at[me * tp + t], rsend.at[k], rrecv.at[me * tp + t],
+               (peer // tp, peer % tp)).wait_send()
+        return carry
+
+    lax.fori_loop(1, seq * tp, wait_rel, 0)
+    relsum_ref[...] = jnp.sum(relbuf[...], axis=0)
+
+    give.wait_recv()
+    mixed_ref[...] = ours + rbuf[...].astype(jnp.float32)
+
+    for copy in pending:
+        copy.wait_send()
+    for k in range(hloc):
+        hl_k = lax.rem(me + k, hloc)
+        same_k = jnp.logical_and(t * hloc + hl_k == me, wcore == t)
+
+        @pl.when(jnp.logical_not(same_k))
+        def _():
+            remote(w_ref.at[hl_k], wbuf.at[me], wsend.at[k], wrecv.at[me], (t * hloc + hl_k, wcore)).wait_send()
+
+    @pl.when(home != t)
+    def _():
+        remote(attsrc.at[me], mine, asend.at[0], arecv.at[hl * 2 + t], (me, home)).wait_send()
+
+
+def head_call(n, seq, tp, half_img, cid, chunk, w_heads, wout, gain, mask, rel):
+    cols = 4
+    planes = seq // cols
+    groups = 4
+    hloc, depth, three = w_heads.shape
+    rows, width = chunk.shape[1:]
+    dims = (seq, tp, hloc, cols, half_img, groups)
+    out_rows, out_width = n * half_img * tp, wout.shape[1] // tp
+    dma = pltpu.SemaphoreType.DMA
+    bf16 = jnp.bfloat16
+    vmem = pl.BlockSpec(memory_space=pltpu.VMEM)
+    hbm = pl.BlockSpec(memory_space=pl.ANY)
+    return pl.pallas_call(
+        functools.partial(head_kernel, n, dims),
+        out_shape=(
+            jax.ShapeDtypeStruct((out_rows, out_width), jnp.float32),
+            jax.ShapeDtypeStruct(rel.shape, jnp.float32),
+        ),
+        in_specs=[vmem, hbm, hbm, vmem, vmem, vmem],
+        out_specs=(vmem, vmem),
+        scratch_shapes=[
+            pltpu.VMEM((seq, 2, rows, width), bf16),
+            pltpu.VMEM((seq, depth, three), bf16),
+            pltpu.VMEM(wout.shape, bf16),
+            pltpu.VMEM((seq, rows, HD), bf16),
+            pltpu.VMEM((tp, seq, 2, rows, HD), bf16),
+            pltpu.VMEM((seq, n * half_img, HD), bf16),
+            pltpu.VMEM((out_rows, hloc * HD), bf16),
+            pltpu.VMEM((out_rows, out_width), bf16),
+            pltpu.VMEM((out_rows, out_width), bf16),
+            pltpu.VMEM((seq * tp,) + rel.shape, jnp.float32),
+            dma((2,)),
+            dma((planes,)),
+            dma((planes, 2)),
+            dma((planes, 2)),
+            dma((seq,)),
+            dma((planes, 2)),
+            dma((hloc,)),
+            dma((seq,)),
+            dma((seq // 2,)),
+            dma((groups,)),
+            dma((groups,)),
+            dma((seq,)),
+            dma((seq,)),
+            dma((1,)),
+            dma((1,)),
+            dma((seq * tp,)),
+            dma((seq * tp,)),
+        ],
+        compiler_params=pltpu.CompilerParams(
+            collective_id=cid, has_side_effects=True, vmem_limit_bytes=58 * 1024 * 1024
+        ),
+    )(chunk, w_heads, wout, gain, mask, rel)
+
+
+def by_heads(seq, tp, img, txt, prev_mod, cache, modulation, w_qkv, qk_gain, output_weight, text_len, refresh):
+    batch, img_rows, width_loc = img.shape
+    txt_rows = txt.shape[1]
+    me, t = lax.axis_index("seq"), lax.axis_index("tp")
+    hloc = w_qkv.shape[2] // HD
+    joined = jnp.concatenate([txt, img], axis=1)
+    local_mods = modulation.astype(jnp.float32)
+    wide = lax.all_gather(joined, "tp", axis=2, tiled=True)
+    n_mod = modulation.shape[0] * batch * width_loc
+    small = jnp.concatenate([local_mods.reshape(n_mod), qk_gain.reshape(-1)])
+    small = lax.all_gather(small, "tp", axis=0)
+    wide_mods = small[:, :n_mod].reshape(tp, 3, batch, width_loc).transpose(1, 2, 0, 3).reshape(3, batch, tp * width_loc)
+    gains = small[:, n_mod:].reshape(tp, 2, hloc, HD).transpose(1, 0, 2, 3).reshape(2, tp * hloc, HD)
+    gain = lax.dynamic_index_in_dim(gains, me, 1, keepdims=False)
+    values = wide.astype(jnp.float32)
+    center = jnp.mean(values, axis=2, keepdims=True)
+    spread = jnp.mean(jnp.square(values - center), axis=2, keepdims=True)
+    scale = lax.rsqrt(spread + EPS)
+
+    def modulate(block, mid, inv, mods):
+        return ((block - mid) * inv * (1.0 + mods[1][:, None, :]) + mods[0][:, None, :]).astype(jnp.bfloat16)
+
+    own_image = modulate(img.astype(jnp.float32), center[:, txt_rows:], scale[:, txt_rows:], local_mods)
+    previous = prev_mod.astype(jnp.float32)
+    gap = jnp.sum(jnp.abs(own_image.astype(jnp.float32) - previous), axis=(1, 2))
+    base_sum = jnp.sum(jnp.abs(previous), axis=(1, 2))
+    rel = jnp.broadcast_to(jnp.stack([gap, base_sum]).reshape(2 * batch, 1), (2 * batch, 128))
+
+    on = refresh == 1
+    rank = jnp.cumsum(on.astype(jnp.int32)) - on.astype(jnp.int32)
+    w_heads = w_qkv.reshape(w_qkv.shape[0], 3, hloc, HD).transpose(2, 0, 1, 3).reshape(hloc, w_qkv.shape[0], 3 * HD)
+    half_img, half_txt = img_rows // tp, txt_rows // tp
+
+    def run(n, cid):
+        slots = jnp.arange(n, dtype=jnp.int32)
+        hit = on[None, :] & (rank[None, :] == slots[:, None])
+        sel = jnp.sum(jnp.where(hit, jnp.arange(batch, dtype=jnp.int32)[None, :], 0), axis=1)
+        pad = -(-n * half_txt // 16) * 16
+        rows_i = lax.dynamic_slice_in_dim(values, txt_rows + t * half_img, half_img, 1)
+        rows_t = lax.dynamic_slice_in_dim(values, t * half_txt, half_txt, 1)
+        mid_i = lax.dynamic_slice_in_dim(center, txt_rows + t * half_img, half_img, 1)
+        mid_t = lax.dynamic_slice_in_dim(center, t * half_txt, half_txt, 1)
+        inv_i = lax.dynamic_slice_in_dim(scale, txt_rows + t * half_img, half_img, 1)
+        inv_t = lax.dynamic_slice_in_dim(scale, t * half_txt, half_txt, 1)
+        mod_i = modulate(rows_i, mid_i, inv_i, wide_mods)
+        mod_t = modulate(rows_t, mid_t, inv_t, wide_mods)
+        pick = lambda a: jnp.concatenate([lax.dynamic_slice_in_dim(a, sel[i], 1, 0) for i in range(n)], axis=0)
+        mod_i = pick(mod_i).reshape(n * half_img, -1)
+        mod_t = pick(mod_t).reshape(n * half_txt, -1)
+        mod_t = jnp.pad(mod_t, ((0, pad - n * half_txt), (0, 0)))
+        chunk = jnp.concatenate([mod_i, mod_t], axis=0)
+        chunk = jnp.stack([chunk[:, :width_loc], chunk[:, width_loc:]])
+        r = jnp.arange(pad, dtype=jnp.int32)
+        pos = (jnp.arange(seq, dtype=jnp.int32)[None, :, None] * txt_rows
+               + jnp.arange(tp, dtype=jnp.int32)[:, None, None] * half_txt + (r % half_txt)[None, None, :])
+        lens = jnp.stack([lax.dynamic_index_in_dim(text_len, sel[i], 0, keepdims=False) for i in range(n)])
+        ok_t = ((r // half_txt)[None, None, None, :] == slots[:, None, None, None]) & (pos[None] < lens[:, None, None, None])
+        ok_t = ok_t.reshape(n, tp, seq * pad)
+        ok_i = jnp.ones((n, tp, seq * half_img), bool)
+        mask = jnp.concatenate([ok_i, ok_t], axis=2).reshape(n, -1).astype(jnp.float32)
+        mixed, sums = head_call(n, seq, tp, half_img, cid, chunk, w_heads, output_weight, gain, mask, rel)
+        mixed = mixed.reshape(tp, n, half_img, width_loc).transpose(1, 0, 2, 3).reshape(n, img_rows, width_loc)
+        back = jnp.minimum(rank, n - 1)
+        whole = jnp.concatenate([lax.dynamic_slice_in_dim(mixed, back[b], 1, 0) for b in range(batch)], axis=0)
+        resid = local_mods[2][:, None, :] * whole
+        new_cache = jnp.where(on[:, None, None], resid, cache)
+        out_img = img.astype(jnp.float32) + new_cache
+        numer, denom = sums[:batch, 0], sums[batch:, 0]
+        return out_img, new_cache, numer / jnp.maximum(denom, 1.0)
+
+    return run(batch - 1, 0)
+
+
 def solution(mesh):
+    seq, tp = mesh.shape["seq"], mesh.shape["tp"]
+
+    def step(*args):
+        img, txt, w_qkv = args[0], args[1], args[5]
+        hloc = w_qkv.shape[2] // HD
+        fits = (
+            tp == 2 and seq % 8 == 0 and hloc * tp == seq and img.shape[0] == 4
+            and img.shape[1] % 32 == 0 and txt.shape[1] % 2 == 0
+        )
+        if fits:
+            return by_heads(seq, tp, *args)
+        return local(*args)
+
     return jax.shard_map(
-        local,
+        step,
         mesh=mesh,
         in_specs=(
             P(None, "seq", "tp"),

time: 436 us -> 157 us (0.36)
  waiting for transfers between devices: 302 us -> 0 us
  Pallas kernels: 0 us -> 120 us
  blocking collectives: 46 us -> 4.43 us
  matrix products: 25.6 us -> 0 us
  local copies, waits for them, and re-layouts: 34.7 us -> 9.69 us
    all_gather x2 -> x0, waiting for transfers between devices: 284 us -> none  [the longest x1 208 us: local(): lax.all_gather(w_qkv, 'seq', axis=0, tiled=True)]
    pallas_call x0 -> x1, Pallas kernels: none -> 120 us  [head_call(): pl.pallas_call(functools.partial(head_kernel, n, dims), out_shape=(jax.Sh...]
    psum x1 -> x0, blocking collectives: 41.4 us -> none  [local(): numer, denom = lax.psum((gap, base_sum), ('seq', 'tp'))]
    dot_general x4 -> x0, matrix products: 25.6 us -> none  [the longest x1 8.14 us: local(): jnp.einsum('btd,dkc->btkc', modded, lax.all_gather(w_qkv, 'seq', axis=0,...]
    psum x1 -> x0, waiting for transfers between devices: 17.8 us -> none  [local(): lax.psum(partial_output.astype(jnp.bfloat16), 'tp').astype(jnp.float32)]
    another operation x3, local copies, waits for them, and re-layouts: 17.4 us -> 0.18 us  [the longest x1 8.05 us: local(): vals = piece[:, :, 1, :].reshape(batch, count, heads, HD)]
    slice x5 -> x3, local copies, waits for them, and re-layouts: 12.6 us -> 1.26 us  [the longest x1 0.66 us: run(): back[b]]
  transfers between devices with their start and end apart: 3 -> 0, of which waited for: 3 -> 0; matrix products, arithmetic and copies ran while one was open for 2% -> 0% of each run, Pallas kernels for 0% -> 0%
where the time goes in v1:
time: 157 us
  Pallas kernels  120 us (76%)
  between operations  14.6 us (9%)
  local copies, waits for them, and re-layouts  9.69 us (6%)
  other arithmetic  8.36 us (5%)
  blocking collectives  4.43 us (3%)
    pallas_call x1, Pallas kernels, head_call(): pl.pallas_call(functools.partial(head_kernel, n, dims), out_shape=(jax.Sh...  120 us
    reshape x2, local copies, waits for them, and re-layouts, by_heads(): w_qkv.reshape(w_qkv.shape[0], 3, hloc, HD).transpose(2, 0, 1, 3)  3.24 us

profile of v1, /device:TPU:1, one launch (start us, length us, event | category | flops | bytes accessed | tf_op | source)
XLA Modules:
  0.0 156.9 jit_solution(6411169490113308092)
XLA Ops:
  0.6 1.1 pad_maximum_fusion
  1.8 2.5 %all_gather.9 = bf16[4,36,3072]{2,1,0:T(8,128)(2,1)S(1)} all-gather(bf16[4,36,1536]{2,1,0:T(8,128)(2,1)S(1)} %pad_maximum_fusion), channel_id=1, replica_groups=mesh['seq'=16,'tp'=2] {'tp'}, dimensions={2}, use_global_device_ids=true | all-gather | bytes 1327104 | tf_op jit(solution)/shard_map/all_gather | solution.py:384
  4.3 0.2 convert_reduce_fusion
  4.5 0.0 copy-start.4
  4.5 0.0 copy-start.5
  4.5 0.4 multiply_reduce_fusion
  5.0 0.1 constant_dynamic-slice_fusion.13
  5.0 0.2 convert_element_type.38
  5.2 0.0 copy-done.4
  5.3 0.0 copy-start.8
  5.3 0.0 copy-done.5
  5.3 1.9 %all-gather = f32[40960]{0:T(1024)S(1)} all-gather(f32[20480]{0:T(1024)S(1)} %pad_maximum_fusion.3), channel_id=2, replica_groups=mesh['seq'=16,'tp'=2] {'tp'}, dimensions={0}, use_global_device_ids=true | all-gather | bytes 245760 | tf_op jit(solution)/shard_map/all_gather | solution.py:387
  7.3 0.1 reshape.249
  7.4 0.2 reshape.237
  7.6 0.2 add_convert_fusion
  7.8 0.0 copy-done.8
  7.8 0.2 reduce-window.9
  8.0 0.1 select_reduce_fusion
  8.1 0.6 fusion.19
  14.5 0.0 copy-start.6
  14.6 0.0 copy-start
  14.6 0.0 copy-start.3
  14.7 0.1 constant_dynamic-slice_fusion.8
  14.7 0.1 add_convert_fusion.1
  14.9 0.0 copy-start.1
  14.9 0.1 pad_maximum_fusion.4
  15.1 0.8 pad_maximum_fusion.1.chunk_ref
  15.9 0.0 copy-done.6
  15.9 0.7 fusion.18
  16.5 2.0 %pad_add_fusion = s32[3]{0:T(128)S(1)} fusion(s32[1]{0:T(128)} %get-tuple-element.39, s32[1]{0:T(128)} %get-tuple-element.40, s32[1]{0:T(128)} %get-tuple-element.38), kind=kLoop, calls=%fused_computation.72 | loop fusion | flops 6 | bytes 24 | tf_op jit(solution)/shard_map/stack | solution.py:432
  18.6 0.1 add.202
  18.7 0.1 broadcast_add_fusion.1
  18.8 0.1 add.198
  18.8 0.1 add.199
  19.0 0.1 and.52
  19.1 0.1 compare_and_fusion
  19.1 0.6 copy.29
  19.8 0.1 slice_bitcast_fusion.5
  19.9 0.0 copy-done
  19.9 0.0 copy-done.3
  19.9 0.4 fusion.5
  20.3 0.1 broadcast_in_dim.24
  20.4 0.7 broadcast_in_dim.25.rel_ref
  21.1 0.6 constant_dynamic-slice_fusion.4
  21.7 0.0 copy-done.1
  21.7 0.3 copy.27
  22.0 1.0 copy.35
  23.0 2.2 %reshape.243.w_ref = bf16[8,192,384]{2,1,0:T(8,128)(2,1)} reshape(bf16[8,192,3,128]{3,2,1,0:T(4,128)(2,1)S(1)} %bitcast.68) | data formatting | bytes 2359296 | tf_op jit(solution)/shard_map/reshape | solution.py:407
  25.2 119.8 %shard_map.121 = (f32[96,1536]{1,0:T(8,128)}, f32[8,128]{1,0:T(8,128)}) custom-call(bf16[2,64,1536]{2,1,0:T(8,128)(2,1)} %pad_maximum_fusion.1.chunk_ref, bf16[8,192,384]{2,1,0:T(8,128)(2,1)} %reshape.243.w_ref, bf16[1024,3072]{1,0:T(8,128)(2,1)} %wout_ref.1, f32[2,128]{1,0:T(2,128)} %bitcast.82, f32[3,1024]{1,0:T(4,128)} %bitcast.79, ...), custom_call_target="tpu_custom_call" | custom-call | tf_op jit(solution)/shard_map/pallas_call | solution.py:334
  145.1 0.0 copy-start.2
  145.1 1.2 copy.25
  146.2 0.7 fusion.17
  154.8 0.1 constant_dynamic-slice_fusion.3
  154.8 0.0 copy-start.7
  154.8 0.0 copy-done.2
  154.9 1.4 convert_add_fusion
  156.3 0.0 copy-done.7
  156.3 0.6 fusion.13
  (28 shorter events, 0.3 us)
Async XLA Ops:
  4.5 0.8 copy-start.4
  4.5 0.8 copy-start.5
  5.3 2.5 %copy-start.8 = (s32[4]{0:T(128)S(1)}, s32[4]{0:T(128)}, u32[]{:S(2)}) copy-start(s32[4]{0:T(128)} %param.19) | copy-start | bytes 52
  14.5 1.4 copy-start.6
  14.6 5.3 %copy-start = (bf16[4,32,1536]{2,1,0:T(8,128)(2,1)S(1)}, bf16[4,32,1536]{2,1,0:T(8,128)(2,1)}, u32[]{:S(2)}) copy-start(bf16[4,32,1536]{2,1,0:T(8,128)(2,1)} %param.10) | copy-start | bytes 1179652
  14.6 5.3 %copy-start.3 = (bf16[4,32,1536]{2,1,0:T(8,128)(2,1)S(1)}, bf16[4,32,1536]{2,1,0:T(8,128)(2,1)}, u32[]{:S(2)}) copy-start(bf16[4,32,1536]{2,1,0:T(8,128)(2,1)} %param.12) | copy-start | bytes 1179652
  14.9 6.8 %copy-start.1 = (bf16[192,3,1024]{2,0,1:T(8,128)(2,1)S(1)}, bf16[192,3,1024]{2,0,1:T(8,128)(2,1)}, u32[]{:S(2)}) copy-start(bf16[192,3,1024]{2,0,1:T(8,128)(2,1)} %param.15) | copy-start | bytes 3538948
  145.1 9.8 %copy-start.2 = (f32[4,32,1536]{2,1,0:T(8,128)S(1)}, f32[4,32,1536]{2,1,0:T(8,128)}, u32[]{:S(2)}) copy-start(f32[4,32,1536]{2,1,0:T(8,128)} %param.13) | copy-start | bytes 2359300
  154.8 1.4 copy-start.7

commit v2 on v1

--- a/solution.py
+++ b/solution.py
@@ -410,8 +410,7 @@
     def run(n, cid):
         slots = jnp.arange(n, dtype=jnp.int32)
         hit = on[None, :] & (rank[None, :] == slots[:, None])
-        sel = jnp.sum(jnp.where(hit, jnp.arange(batch, dtype=jnp.int32)[None, :], 0), axis=1)
-        pad = -(-n * half_txt // 16) * 16
+        pad = -(-n * half_txt // 8) * 8
         rows_i = lax.dynamic_slice_in_dim(values, txt_rows + t * half_img, half_img, 1)
         rows_t = lax.dynamic_slice_in_dim(values, t * half_txt, half_txt, 1)
         mid_i = lax.dynamic_slice_in_dim(center, txt_rows + t * half_img, half_img, 1)
@@ -420,7 +419,13 @@
         inv_t = lax.dynamic_slice_in_dim(scale, t * half_txt, half_txt, 1)
         mod_i = modulate(rows_i, mid_i, inv_i, wide_mods)
         mod_t = modulate(rows_t, mid_t, inv_t, wide_mods)
-        pick = lambda a: jnp.concatenate([lax.dynamic_slice_in_dim(a, sel[i], 1, 0) for i in range(n)], axis=0)
+
+        def pick(a):
+            taken = a[batch - 1][None]
+            for b in range(batch - 1):
+                taken = jnp.where(hit[:, b, None, None], a[b][None], taken)
+            return taken
+
         mod_i = pick(mod_i).reshape(n * half_img, -1)
         mod_t = pick(mod_t).reshape(n * half_txt, -1)
         mod_t = jnp.pad(mod_t, ((0, pad - n * half_txt), (0, 0)))
@@ -429,22 +434,25 @@
         r = jnp.arange(pad, dtype=jnp.int32)
         pos = (jnp.arange(seq, dtype=jnp.int32)[None, :, None] * txt_rows
                + jnp.arange(tp, dtype=jnp.int32)[:, None, None] * half_txt + (r % half_txt)[None, None, :])
-        lens = jnp.stack([lax.dynamic_index_in_dim(text_len, sel[i], 0, keepdims=False) for i in range(n)])
+        lens = jnp.sum(jnp.where(hit, text_len[None, :], 0), axis=1)
         ok_t = ((r // half_txt)[None, None, None, :] == slots[:, None, None, None]) & (pos[None] < lens[:, None, None, None])
         ok_t = ok_t.reshape(n, tp, seq * pad)
         ok_i = jnp.ones((n, tp, seq * half_img), bool)
         mask = jnp.concatenate([ok_i, ok_t], axis=2).reshape(n, -1).astype(jnp.float32)
         mixed, sums = head_call(n, seq, tp, half_img, cid, chunk, w_heads, output_weight, gain, mask, rel)
         mixed = mixed.reshape(tp, n, half_img, width_loc).transpose(1, 0, 2, 3).reshape(n, img_rows, width_loc)
-        back = jnp.minimum(rank, n - 1)
-        whole = jnp.concatenate([lax.dynamic_slice_in_dim(mixed, back[b], 1, 0) for b in range(batch)], axis=0)
-        resid = local_mods[2][:, None, :] * whole
-        new_cache = jnp.where(on[:, None, None], resid, cache)
-        out_img = img.astype(jnp.float32) + new_cache
-        numer, denom = sums[:batch, 0], sums[batch:, 0]
-        return out_img, new_cache, numer / jnp.maximum(denom, 1.0)
-
-    return run(batch - 1, 0)
+        whole = mixed[n - 1][None]
+        for k in range(n - 1):
+            whole = jnp.where((rank == k)[:, None, None], mixed[k][None], whole)
+        return jnp.broadcast_to(whole, img.shape), sums
+
+    level = jnp.clip(jnp.sum(on.astype(jnp.int32)) - 1, 0, batch - 2)
+    whole, sums = lax.switch(level, [functools.partial(run, k + 1, k) for k in range(batch - 1)])
+    resid = local_mods[2][:, None, :] * whole
+    new_cache = jnp.where(on[:, None, None], resid, cache)
+    out_img = img.astype(jnp.float32) + new_cache
+    numer, denom = sums[:batch, 0], sums[batch:, 0]
+    return out_img, new_cache, numer / jnp.maximum(denom, 1.0)
 
 
 def solution(mesh):

time: 157 us -> 153 us (0.975)
  Pallas kernels: 120 us -> 85.2 us
  local copies, waits for them, and re-layouts: 9.69 us -> 40.2 us
  between operations: 14.6 us -> 1.39 us
  other arithmetic: 8.36 us -> 20 us
    pallas_call x1, Pallas kernels: 120 us -> 85.2 us  [head_call(): pl.pallas_call(functools.partial(head_kernel, n, dims), out_shape=(jax.Sh...]
    broadcast_in_dim x0 -> x23, local copies, waits for them, and re-layouts: none -> 14.7 us  [pick(): taken = jnp.where(hit[:, b, None, None], a[b][None], taken)]
    add x4, local copies, waits for them, and re-layouts: 0.24 us -> 4.78 us  [run(): jnp.arange(seq, dtype=jnp.int32)[None, :, None] * txt_rows]
    sub x0 -> x2, local copies, waits for them, and re-layouts: none -> 2.6 us  [modulate(): block - mid]
    reshape x2, local copies, waits for them, and re-layouts: 3.24 us -> 5.55 us  [by_heads(): w_qkv.reshape(w_qkv.shape[0], 3, hloc, HD).transpose(2, 0, 1, 3)]
    another operation x2 -> x1, other arithmetic: 2.22 us -> 0.18 us  [the longest x1 2.05 us: run(): jnp.stack([lax.dynamic_index_in_dim(text_len, sel[i], 0, keepdims=False)...]
    dynamic_slice x4 -> x3, local copies, waits for them, and re-layouts: 0.79 us -> 2.75 us  [the longest x2 2.1 us: run(): lax.dynamic_slice_in_dim(scale, txt_rows + t * half_img, half_img, 1)]
    sub x0 -> x1, other arithmetic: none -> 1.8 us  [by_heads(): rank = jnp.cumsum(on.astype(jnp.int32)) - on.astype(jnp.int32)]
where the time goes in v2:
time: 153 us; the launch traced here: 152 us
  Pallas kernels  85.2 us (56%)
  local copies, waits for them, and re-layouts  40.2 us (26%)
  other arithmetic  20 us (13%)
  blocking collectives  4.55 us (3%)
    pallas_call x1, Pallas kernels, head_call(): pl.pallas_call(functools.partial(head_kernel, n, dims), out_shape=(jax.Sh...  85.2 us
    broadcast_in_dim x23, local copies, waits for them, and re-layouts, pick(): taken = jnp.where(hit[:, b, None, None], a[b][None], taken)  14.7 us
    reshape x2, local copies, waits for them, and re-layouts, by_heads(): w_qkv.reshape(w_qkv.shape[0], 3, hloc, HD).transpose(2, 0, 1, 3)  5.55 us
    add x4, local copies, waits for them, and re-layouts, run(): jnp.arange(seq, dtype=jnp.int32)[None, :, None] * txt_rows  4.78 us

profile of v2, /device:TPU:1, one launch (start us, length us, event | category | flops | bytes accessed | tf_op | source)
XLA Modules:
  0.0 152.1 jit_solution(8213307771673517067)
XLA Ops:
  0.6 1.3 broadcast_compare_fusion.3
  1.9 0.2 reduce-window.9
  2.1 1.8 %bitcast_subtract_fusion = (s32[4]{0:T(128)}, s32[]{:T(128)}) fusion(s32[4,1]{0,1:T(1,128)S(1)} %reduce-window.9, s32[4]{0:T(128)} %param.22), kind=kLoop, calls=%fused_computation.170 | loop fusion | flops 15 | bytes 52 | tf_op jit(solution)/shard_map/sub | solution.py:406
  4.6 0.7 copy.97
  5.3 0.8 reshape.568
  6.1 0.8 convert_element_type.64
  6.8 0.6 slice_bitcast_fusion.32
  7.4 1.9 %all-gather = f32[40960]{0:T(1024)S(1)} all-gather(f32[20480]{0:T(1024)S(1)} %pad_maximum_fusion.4), channel_id=2, replica_groups=mesh['seq'=16,'tp'=2] {'tp'}, dimensions={0}, use_global_device_ids=true | all-gather | bytes 245760 | tf_op jit(solution)/shard_map/all_gather | solution.py:387
  9.5 0.8 reshape.571
  10.3 0.9 pad_maximum_fusion.3
  11.3 2.6 %all_gather.9 = bf16[4,36,3072]{2,1,0:T(8,128)(2,1)S(1)} all-gather(bf16[4,36,1536]{2,1,0:T(8,128)(2,1)S(1)} %pad_maximum_fusion.3), channel_id=1, replica_groups=mesh['seq'=16,'tp'=2] {'tp'}, dimensions={2}, use_global_device_ids=true | all-gather | bytes 1327104 | tf_op jit(solution)/shard_map/all_gather | solution.py:384
  13.9 0.2 convert_reduce_fusion
  14.1 0.4 multiply_reduce_fusion
  14.6 0.5 fusion.32
  15.3 0.2 convert_element_type.66
  15.5 1.6 %copy.89 = bf16[72,8,8,128]{3,2,1,0:T(8,128)(2,1)S(1)} copy(bf16[72,8,8,128]{3,1,2,0:T(8,128)(2,1)} %bitcast.189) | data formatting | bytes 2359296
  17.1 2.2 %copy.96 = bf16[192,3,8,128]{3,1,0,2:T(4,128)(2,1)} copy(bf16[192,3,8,128]{3,2,0,1:T(8,128)(2,1)S(1)} %bitcast.188) | data formatting | bytes 2359296 | tf_op jit(solution)/shard_map/reshape | solution.py:407
  19.3 3.4 %reshape.573 = bf16[8,192,384]{2,1,0:T(8,128)(2,1)S(1)} reshape(bf16[8,192,3,128]{3,2,1,0:T(4,128)(2,1)} %bitcast.187) | data formatting | bytes 2359296 | tf_op jit(solution)/shard_map/reshape | solution.py:407
  22.6 126.3 %conditional.1 = (f32[4,32,1536]{2,1,0:T(8,128)S(1)}, f32[8,128]{1,0:T(8,128)S(1)}) conditional(s32[]{:T(128)} %clamp.3, (s32[4]{0:T(128)}, pred[4]{0:T(512)(128)(4,1)}, s32[]{:T(128)}, f32[4,36,3072]{2,1,0:T(8,128)S(1)}, f32[4,36,1]{1,0,2:T(4,128)S(1)}, /*index=5*/f32[4,36,1]{1,0,2:T(4,128)S(1)}, f32[3,4,3072]{2,1,0:T(4,128)}, ...), branch_computations={%region_6.8_spmd, %region_8.10_spmd, %region_10.12_spmd} | conditional | flops 3217640 | bytes 8623368 | solution.py:450
  22.7 1.2 broadcast_compare_fusion
  23.9 1.3 select_reduce_fusion.1
  25.2 0.7 broadcast_add_fusion.2
  25.9 0.6 and_select_fusion.2
  26.4 0.5 iota_compare_fusion.3
  27.0 0.6 slice_bitcast_fusion.16
  27.5 0.6 broadcast_in_dim.429
  28.2 0.7 broadcast_in_dim.406
  28.9 1.3 broadcast_in_dim.407
  30.1 1.3 broadcast_in_dim.430
  31.5 1.2 broadcast_in_dim.441
  32.7 1.3 broadcast_in_dim.420
  34.0 1.3 broadcast_in_dim.421
  35.3 1.3 broadcast_in_dim.442
  36.5 1.2 broadcast_in_dim.435
  37.8 1.2 broadcast_in_dim.413
  39.0 1.3 broadcast_in_dim.414
  40.2 1.2 broadcast_in_dim.436
  41.5 0.6 and.129
  42.1 0.6 and.130
  42.7 1.3 add.326
  44.0 1.4 add.327
  45.4 1.4 add.323
  46.7 0.8 add.324
  47.5 0.7 broadcast_add_fusion.1
  48.2 0.7 compare_and_fusion.2
  48.9 0.6 copy.86
  49.5 0.7 copy.82
  50.2 0.7 copy.81
  50.9 1.3 fusion.17
  52.2 1.3 constant_dynamic-slice_fusion.6
  53.5 0.8 copy.69
  54.3 1.3 copy.70
  55.6 1.3 copy.71
  56.9 0.7 copy.68
  57.5 0.8 add_bitcast_fusion.1
  58.4 0.8 add_convert_fusion.3
  59.2 0.9 add_convert_fusion.2
  60.6 0.7 select_select_fusion
  61.3 0.7 pad_maximum_fusion.1.chunk_ref
  62.0 85.2 %branch_1_fun.1 = (f32[64,1536]{1,0:T(8,128)}, f32[8,128]{1,0:T(8,128)S(1)}) custom-call(bf16[2,40,1536]{2,1,0:T(8,128)(2,1)} %pad_maximum_fusion.1.chunk_ref, bf16[8,192,384]{2,1,0:T(8,128)(2,1)S(1)} %get-tuple-element.93.w_ref, bf16[1024,3072]{1,0:T(8,128)(2,1)} %get-tuple-element.94.wout_ref, f32[2,128]{1,0:T(2,128)S(1)} %copy-done.3, ...), custom_call_target="tpu_custom_call" | custom-call | tf_op jit(solution)/shard_map/cond/branch_1_fun/pallas_call | solution.py:334
  147.2 1.1 fusion.40
  148.3 0.1 broadcast_select_fusion.3
  148.9 0.6 fusion.35
  149.6 2.6 %convert_add_fusion = (f32[4,32,1536]{2,1,0:T(8,128)}, f32[4,32,1536]{2,1,0:T(8,128)}) fusion(bf16[4,32,1536]{2,1,0:T(8,128)(2,1)S(1)} %copy-done, f32[4,32,1536]{2,1,0:T(8,128)} %param.16, f32[4,32,1536]{2,1,0:T(8,128)S(1)} %get-tuple-element.119, f32[4,1536]{1,0:T(4,128)} %get-tuple-element.225, pred[4]{0:T(512)(128)(4,1)} %get-tuple-element.230), kind=kLoop, calls=%fused_computation.143 | loop fusion | flops 786432 | bytes 3563524 | tf_op jit(solution)/shard_map/add | solution.py:453
  (48 shorter events, 0.8 us)
Async XLA Ops:
  0.6 9.7 %copy-start = (bf16[4,32,1536]{2,1,0:T(8,128)(2,1)S(1)}, bf16[4,32,1536]{2,1,0:T(8,128)(2,1)}, u32[]{:S(2)}) copy-start(bf16[4,32,1536]{2,1,0:T(8,128)(2,1)} %param.13) | copy-start | bytes 1179652
  11.2 3.4 %copy-start.1 = (bf16[4,32,1536]{2,1,0:T(8,128)(2,1)S(1)}, bf16[4,32,1536]{2,1,0:T(8,128)(2,1)}, u32[]{:S(2)}) copy-start(bf16[4,32,1536]{2,1,0:T(8,128)(2,1)} %param.15) | copy-start | bytes 1179652
  22.7 17.6 %copy-start.2 = (f32[2,128]{1,0:T(2,128)}, f32[2,128]{1,0:T(2,128)S(1)}, u32[]{:S(2)}) copy-start(f32[2,128]{1,0:T(2,128)S(1)} %get-tuple-element.95.gain_ref) | copy-start | bytes 3076 | tf_op jit(solution)/shard_map/cond
  57.5 2.6 %copy-start.12 = (pred[32]{0:T(512)(128)(4,1)S(1)}, pred[32]{0:T(512)(128)(4,1)}, u32[]{:S(2)}) copy-start(pred[32]{0:T(512)(128)(4,1)} %broadcast_in_dim.407) | copy-start | bytes 100 | tf_op jit(solution)/shard_map/cond
  57.5 2.7 %copy-start.13 = (pred[32]{0:T(512)(128)(4,1)S(1)}, pred[32]{0:T(512)(128)(4,1)}, u32[]{:S(2)}) copy-start(pred[32]{0:T(512)(128)(4,1)} %broadcast_in_dim.421) | copy-start | bytes 100 | tf_op jit(solution)/shard_map/cond
  57.5 2.7 %copy-start.14 = (pred[32]{0:T(512)(128)(4,1)S(1)}, pred[32]{0:T(512)(128)(4,1)}, u32[]{:S(2)}) copy-start(pred[32]{0:T(512)(128)(4,1)} %broadcast_in_dim.414) | copy-start | bytes 100 | tf_op jit(solution)/shard_map/cond
  57.5 3.0 %copy-start.7 = (pred[4]{0:T(512)(128)(4,1)S(1)}, pred[4]{0:T(512)(128)(4,1)}, u32[]{:S(2)}) copy-start(pred[4]{0:T(512)(128)(4,1)} %broadcast_in_dim.430) | copy-start | bytes 16 | tf_op jit(solution)/shard_map/cond
  57.5 3.0 %copy-start.8 = (pred[4]{0:T(512)(128)(4,1)S(1)}, pred[4]{0:T(512)(128)(4,1)}, u32[]{:S(2)}) copy-start(pred[4]{0:T(512)(128)(4,1)} %broadcast_in_dim.442) | copy-start | bytes 16 | tf_op jit(solution)/shard_map/cond
  60.1 1.9 %copy-start.3 = (f32[2,128]{1,0:T(2,128)S(1)}, f32[2,128]{1,0:T(2,128)}, u32[]{:S(2)}) copy-start(f32[2,128]{1,0:T(2,128)} %copy-done.2) | copy-start | bytes 3076 | tf_op jit(solution)/shard_map/cond
  62.0 86.3 %copy-start.4 = (pred[4]{0:T(512)(128)(4,1)S(1)}, pred[4]{0:T(512)(128)(4,1)}, u32[]{:S(2)}) copy-start(pred[4]{0:T(512)(128)(4,1)} %broadcast_compare_fusion) | copy-start | bytes 16 | tf_op jit(solution)/shard_map/cond
